TPU v7x, 32 devices: a whole 2x2x4 slice. The times are simulated.
32 devices in a mesh: rep: 2 (over x), dp: 16 (over y, z, core).
Axes of the slice: x: 2, y: 2, z: 4, core: 2. Of those that a mesh axis runs over, the one named last changes fastest.
Arguments:
- a: bfloat16 [32, 4, 4096, 1280], P(('rep', 'dp')), parts along dimension 0
- g: bfloat16 [32, 4, 4096, 5120], P(('rep', 'dp')), parts along dimension 0
Outputs:
- output: bfloat16 [8, 1280, 5120], P('rep'), parts along dimension 0
There are 2 independent parts. A program takes and returns all parts, laid end to end along the dimension named above; each array names one.
All inputs are finite; a program needn't handle non-finite values.
Results may differ from a plain program's by a relative error of at most 0.012.
Values are sent between devices in bfloat16 or wider.
A program may use at most 2 GiB of HBM per device.

v0:
```python
import jax
import jax.numpy as jnp


def solution(mesh):
    groups = mesh.shape["rep"]

    def step(a, g):
        a, g = (t.reshape(groups, -1, *t.shape[1:]) for t in (a, g))
        sums = jnp.einsum("rsntd,rsntf->rndf", a, g, preferred_element_type=jnp.float32)
        return sums.astype(jnp.bfloat16).reshape(-1, *sums.shape[2:])

    return step
```

profile of v0, /device:TPU:0, one launch (start us, length us, event | category | flops | bytes accessed | tf_op | source)
XLA Modules:
  0.0 2385.4 jit_solution(4222362741804752870)
XLA Ops:
  0.0 234.6 %fusion.2 = f32[1,4,1280,5120]{3,2,1,0:T(8,128)} fusion(bf16[1,4,4096,5120]{3,2,1,0:T(8,128)(2,1)} %param.1, bf16[1,4,4096,1280]{3,2,1,0:T(8,128)(2,1)} %param), kind=kOutput, calls=%fused_computation.2 | convolution fusion | flops 214748364800 | bytes 314572800 | tf_op jit(solution)/rsntd,rsntf->rndf/dot_general | solution.py:10
  234.6 2150.8 %all-reduce.2 = bf16[1,4,1280,5120]{3,2,1,0:T(8,128)(2,1)} all-reduce(f32[1,4,1280,5120]{3,2,1,0:T(8,128)} %fusion.2), channel_id=1, replica_groups=[2,16]<=[32], use_global_device_ids=true, to_apply=%add.clone | all-reduce | flops 26214400 | bytes 157286400 | tf_op jit(solution)/rsntd,rsntf->rndf/dot_general | solution.py:10
where the time goes:
time: 2390 us
  blocking collectives  2150 us (90%)
  matrix products  235 us (10%)
    dot_general x1, blocking collectives, step(): jnp.einsum('rsntd,rsntf->rndf', a, g, preferred_element_type=jnp.float32)  2150 us
    dot_general x1, matrix products, step(): jnp.einsum('rsntd,rsntf->rndf', a, g, preferred_element_type=jnp.float32)  235 us

commit v1 on v0

v1 whole, which is shorter than its diff:
```python
import jax
import jax.numpy as jnp
from jax import lax
from jax.experimental import pallas as pl
from jax.experimental.pallas import tpu as pltpu
from jax.sharding import PartitionSpec as P

MESH = pl.DeviceIdType.MESH
CHIPS_Z = 4
LEFT, RIGHT, ACROSS, PAIR = range(4)

SPLIT = 2
COLS = 256
A_STEP = 256
LAG0 = 2
LAG = 3
STAGES = 8
RING = LAG0 + LAG * STAGES + 3
SUMS = LAG0 + LAG * (STAGES // 2) + 1


def flag(condition):
    return jnp.where(condition, jnp.int32(1), jnp.int32(0))


def role(unit, y, z):
    turn = lax.rem(unit, jnp.int32(10))
    half = turn // 5
    kind = turn - 5 * half
    across_first = kind < 3
    odd = lax.rem(turn, jnp.int32(2))
    root_z = jnp.where(across_first, 1 + odd, 2 * half + kind - 3)
    root_y = jnp.where(across_first, lax.rem(turn // 2, jnp.int32(2)), odd)
    below, above, same = z < root_z, z > root_z, z == root_z
    home = y == root_y
    far = 3 - z
    height = jnp.maximum(root_z, 3 - root_z) + 1
    along = jnp.where(below, z, far)
    level = jnp.where(
        across_first,
        jnp.where(home, jnp.where(same, height, 1 + along), 0),
        jnp.where(same, jnp.where(home, height, height - 1), along),
    )
    depth = jnp.abs(z - root_z) + flag(~home)
    in_line = home | ~across_first
    return dict(
        level=level,
        down=height + depth,
        root=home & same,
        up_right=in_line & below,
        up_left=in_line & above,
        up_across=~home & (across_first | same),
        from_left=in_line & (z <= root_z) & (z > 0),
        from_right=in_line & (z >= root_z) & (z < CHIPS_Z - 1),
        from_across=home & (across_first | same),
    )


def kernel(
    a_hbm, g_hbm, out_hbm,
    a_t, a_in, g_in, product, sums, outgoing, arrived, final,
    a_sem, g_sem, outgoing_sem, arrived_sem, climb_sem, final_sem, leave_sem, other_sem,
):
    matrices, tokens, d = a_hbm.shape
    ff = g_hbm.shape[2]
    rows = d // (2 * SPLIT)
    blocks = ff // COLS
    steps = blocks * SPLIT
    units = matrices * steps
    chunks = tokens // A_STEP

    rep, me = lax.axis_index("rep"), lax.axis_index("dp")
    core = lax.rem(me, 2)
    chip = me // 2
    z = lax.rem(chip, CHIPS_Z)
    y = chip // CHIPS_Z
    partner = me + 1 - 2 * core
    across = me + 2 * CHIPS_Z * (1 - 2 * y)

    def device(i):
        return (rep, i)

    barrier = pltpu.get_barrier_semaphore()

    def greet(i):
        pl.semaphore_signal(barrier, inc=1, device_id=device(i), device_id_type=MESH)

    greet(partner)
    greet(across)

    @pl.when(z > 0)
    def _():
        greet(me - 2)

    @pl.when(z < CHIPS_Z - 1)
    def _():
        greet(me + 2)

    def a_copy(n, i, slot):
        return pltpu.make_async_copy(
            a_hbm.at[n, pl.ds(pl.multiple_of(i * A_STEP, A_STEP), A_STEP)], a_in.at[slot], a_sem.at[slot]
        )

    def g_copy(tile):
        n = tile // blocks
        column = pl.multiple_of((tile - n * blocks) * COLS, COLS)
        slot = lax.rem(tile, 3)
        return pltpu.make_async_copy(g_hbm.at[n, :, pl.ds(column, COLS)], g_in.at[slot], g_sem.at[slot])

    def transpose(n, i, slot):
        a_t[lax.rem(n, 2), :, pl.ds(pl.multiple_of(i * A_STEP, A_STEP), A_STEP)] = a_in[slot].T

    def place(unit, of_core):
        tile = unit // SPLIT
        n = tile // blocks
        row = pl.multiple_of((unit - tile * SPLIT) * (2 * rows) + of_core * rows, rows)
        column = pl.multiple_of((tile - n * blocks) * COLS, COLS)
        return out_hbm.at[n, pl.ds(row, rows), pl.ds(column, COLS)]

    def slot_of(unit):
        return lax.rem(unit, RING)

    def pair_copy(unit):
        slot = slot_of(unit)
        return pltpu.make_async_remote_copy(
            src_ref=outgoing.at[slot], dst_ref=arrived.at[PAIR, slot],
            send_sem=outgoing_sem.at[slot], recv_sem=arrived_sem.at[PAIR, slot],
            device_id=device(partner), device_id_type=MESH,
        )

    def climb_copy(unit, side, to):
        slot = slot_of(unit)
        return pltpu.make_async_remote_copy(
            src_ref=arrived.at[PAIR, slot], dst_ref=arrived.at[side, slot],
            send_sem=climb_sem.at[slot], recv_sem=arrived_sem.at[side, slot],
            device_id=device(to), device_id_type=MESH,
        )

    def final_copy(unit, side, to):
        slot = slot_of(unit)
        return pltpu.make_async_remote_copy(
            src_ref=final.at[slot], dst_ref=final.at[slot],
            send_sem=leave_sem.at[side, slot], recv_sem=final_sem.at[slot],
            device_id=device(to), device_id_type=MESH,
        )

    def other_copy(unit, of_core):
        slot = slot_of(unit)
        return pltpu.make_async_remote_copy(
            src_ref=final.at[slot], dst_ref=place(unit, of_core),
            send_sem=leave_sem.at[PAIR, slot], recv_sem=other_sem.at[slot],
            device_id=device(partner), device_id_type=MESH,
        )

    def own_copy(unit):
        slot = slot_of(unit)
        return pltpu.make_async_copy(final.at[slot], place(unit, core), leave_sem.at[4, slot])

    def compute(unit):
        tile = unit // SPLIT
        part = unit - tile * SPLIT
        n = tile // blocks
        step = unit - n * steps

        @pl.when(part == 0)
        def _():
            @pl.when(tile + 2 < matrices * blocks)
            def _():
                g_copy(tile + 2).start()

            g_copy(tile).wait()

        left = a_t[lax.rem(n, 2), pl.ds(pl.multiple_of(part * 2 * rows, 2 * rows), 2 * rows), :]
        product[...] = jnp.dot(left, g_in[lax.rem(tile, 3)], preferred_element_type=jnp.float32)
        slot = slot_of(unit)
        outgoing[slot] = product[pl.ds(pl.multiple_of((1 - core) * rows, rows), rows), :].astype(jnp.bfloat16)
        pair_copy(unit).start()
        sums[lax.rem(unit, SUMS)] = product[pl.ds(pl.multiple_of(core * rows, rows), rows), :]

        @pl.when(n < matrices - 1)
        def _():
            @pl.when(step < chunks)
            def _():
                a_copy(n + 1, step, lax.rem(step, 2)).start()

            @pl.when((step >= 1) & (step <= chunks))
            def _():
                i = step - 1
                a_copy(n + 1, i, lax.rem(i, 2)).wait()
                transpose(n + 1, i, lax.rem(i, 2))

    def climb(unit, r):
        slot = slot_of(unit)
        at = lax.rem(unit, SUMS)
        for side, there, source in (
            (LEFT, r["from_left"], me - 2),
            (RIGHT, r["from_right"], me + 2),
            (ACROSS, r["from_across"], across),
        ):
            @pl.when(there)
            def _():
                climb_copy(unit, side, source).wait_recv()
                sums[at] = sums[at] + arrived[side, slot].astype(jnp.float32)

        pair_copy(unit).wait_recv()
        total = (sums[at] + arrived[PAIR, slot].astype(jnp.float32)).astype(jnp.bfloat16)

        @pl.when(r["root"])
        def _():
            final[slot] = total

        @pl.when(~r["root"])
        def _():
            arrived[PAIR, slot] = total

        for side, there, to in (
            (LEFT, r["up_right"], me + 2),
            (RIGHT, r["up_left"], me - 2),
            (ACROSS, r["up_across"], across),
        ):
            @pl.when(there)
            def _():
                climb_copy(unit, side, to).start()

    def children(unit, r, act):
        for side, there, to in (
            (LEFT, r["from_left"], me - 2),
            (RIGHT, r["from_right"], me + 2),
            (ACROSS, r["from_across"], across),
        ):
            @pl.when(there)
            def _():
                act(final_copy(unit, side, to))

    def descend(unit, r):
        @pl.when(~r["root"])
        def _():
            climb_copy(unit, LEFT, partner).wait_send()
            final_copy(unit, LEFT, partner).wait_recv()

        children(unit, r, lambda copy: copy.start())
        other_copy(unit, core).start()
        own_copy(unit).start()

    def retire(unit):
        r = role(unit, y, z)
        pair_copy(unit).wait_send()
        children(unit, r, lambda copy: copy.wait_send())
        other_copy(unit, core).wait_send()
        own_copy(unit).wait()
        other_copy(unit, 1 - core).wait_recv()

    a_copy(0, 0, 0).start()
    g_copy(0).start()
    g_copy(1).start()

    def first(i, carry):
        @pl.when(i + 1 < chunks)
        def _():
            a_copy(0, i + 1, lax.rem(i + 1, 2)).start()

        a_copy(0, i, lax.rem(i, 2)).wait()
        transpose(0, i, lax.rem(i, 2))
        return carry

    lax.fori_loop(0, chunks, first, 0)
    pl.semaphore_wait(barrier, 2 + flag(z > 0) + flag(z < CHIPS_Z - 1))

    def body(step, carry):
        @pl.when(step >= RING)
        def _():
            retire(step - RING)

        def stage(i, carry):
            k = STAGES - i
            unit = step - LAG0 - LAG * k

            @pl.when((unit >= 0) & (unit < units))
            def _():
                r = role(unit, y, z)

                @pl.when(r["level"] == k)
                def _():
                    climb(unit, r)

                @pl.when(r["down"] == k)
                def _():
                    descend(unit, r)

            return carry

        lax.fori_loop(0, STAGES + 1, stage, 0)

        @pl.when(step < units)
        def _():
            compute(step)

        return carry

    lax.fori_loop(0, units + RING, body, 0)


def solution(mesh):
    def body(a, g):
        a, g = a[0], g[0]
        matrices, tokens, d = a.shape
        ff = g.shape[2]
        rows = d // (2 * SPLIT)
        block = (rows, COLS)
        dma = pltpu.SemaphoreType.DMA
        flops = 2 * matrices * tokens * d * ff
        return pl.pallas_call(
            kernel,
            out_shape=jax.ShapeDtypeStruct((matrices, d, ff), jnp.bfloat16),
            in_specs=[pl.BlockSpec(memory_space=pl.ANY)] * 2,
            out_specs=pl.BlockSpec(memory_space=pl.ANY),
            scratch_shapes=[
                pltpu.VMEM((2, d, tokens), jnp.bfloat16),
                pltpu.VMEM((2, A_STEP, d), jnp.bfloat16),
                pltpu.VMEM((3, tokens, COLS), jnp.bfloat16),
                pltpu.VMEM((2 * rows, COLS), jnp.float32),
                pltpu.VMEM((SUMS, *block), jnp.float32),
                pltpu.VMEM((RING, *block), jnp.bfloat16),
                pltpu.VMEM((4, RING, *block), jnp.bfloat16),
                pltpu.VMEM((RING, *block), jnp.bfloat16),
                dma((2,)),
                dma((3,)),
                dma((RING,)),
                dma((4, RING)),
                dma((RING,)),
                dma((RING,)),
                dma((5, RING)),
                dma((RING,)),
            ],
            compiler_params=pltpu.CompilerParams(
                collective_id=0, has_side_effects=True, vmem_limit_bytes=67_043_328
            ),
            cost_estimate=pl.CostEstimate(
                flops=flops, bytes_accessed=2 * matrices * (tokens + d) * (d + ff), transcendentals=0
            ),
        )(a, g)

    spec = P(("rep", "dp"))
    return jax.shard_map(body, mesh=mesh, in_specs=(spec, spec), out_specs=P("rep"), check_vma=False)
```

time: 2390 us -> 616 us (0.26)
  blocking collectives: 2150 us -> 0 us
  Pallas kernels: 0 us -> 580 us
  matrix products: 235 us -> 0 us
  local copies, waits for them, and re-layouts: 0 us -> 35.7 us
    dot_general x1 -> x0, blocking collectives: 2150 us -> none  [step(): jnp.einsum('rsntd,rsntf->rndf', a, g, preferred_element_type=jnp.float32)]
    pallas_call x0 -> x1, Pallas kernels: none -> 580 us  [body(): pl.pallas_call(kernel, out_shape=jax.ShapeDtypeStruct((matrices, d, ff),...]
    dot_general x1 -> x0, matrix products: 235 us -> none  [step(): jnp.einsum('rsntd,rsntf->rndf', a, g, preferred_element_type=jnp.float32)]
    unnamed x0 -> x1, local copies, waits for them, and re-layouts: none -> 35.7 us
where the time goes in v1:
time: 616 us
  Pallas kernels  580 us (94%)
  local copies, waits for them, and re-layouts  35.7 us (6%)
    pallas_call x1, Pallas kernels, body(): pl.pallas_call(kernel, out_shape=jax.ShapeDtypeStruct((matrices, d, ff),...  580 us
    unnamed x1, local copies, waits for them, and re-layouts  35.7 us

profile of v1, /device:TPU:0, one launch (start us, length us, event | category | flops | bytes accessed | tf_op | source)
XLA Modules:
  0.0 616.1 jit_solution(11991885641610105042)
XLA Ops:
  0.0 580.4 %shard_map.28 = bf16[4,1280,5120]{2,1,0:T(8,128)(2,1)} custom-call(bf16[4,4096,1280]{2,1,0:T(8,128)(2,1)} %bitcast.2, bf16[4,4096,5120]{2,1,0:T(8,128)(2,1)} %bitcast.1.g_hbm), custom_call_target="tpu_custom_call" | custom-call | flops 214748364800 | bytes 275251200 | tf_op jit(solution)/shard_map/pallas_call | solution.py:312
  580.4 35.7 %copy.4 = bf16[4,1280,5120]{2,1,0:T(8,128)(2,1)} copy(bf16[4,1280,5120]{2,1,0:T(8,128)(2,1)} %shard_map.28) | data formatting | bytes 104857600

commit v2 on v1

v2 whole, which is shorter than its diff:
```python
import jax
import jax.numpy as jnp
from jax import lax
from jax.experimental import pallas as pl
from jax.experimental.pallas import tpu as pltpu
from jax.sharding import PartitionSpec as P

MESH = pl.DeviceIdType.MESH
CHIPS_Z = 4
LEFT, RIGHT, ACROSS, PAIR = range(4)

PANELS = 2
COLS = 256
A_STEP = 256
A_SLOTS = 8
LAG0 = 2
LAG = 4
STAGES = 8
RING = LAG0 + LAG * STAGES + 3
QUEUE = 4
SUMS = LAG0 + LAG * (STAGES // 2) + 1


TREES = (
    (1, 2, 1), (0, 3, 0), (0, 0, 0), (1, 2, 1), (1, 1, 0),
    (0, 1, 0), (1, 2, 0), (0, 2, 1), (1, 1, 0), (1, 2, 1),
)


FLAGS = "root", "up_right", "up_left", "up_across", "from_left", "from_right", "from_across"
UP, DOWN = 1, 2


def flag(condition):
    return jnp.where(condition, jnp.int32(1), jnp.int32(0))


def div(x, by):
    return lax.div(x, jnp.int32(by))


def role(tree, y, z):
    across_first, root_z, root_y = tree
    below, above, same = z < root_z, z > root_z, z == root_z
    home = y == root_y
    height = max(root_z, 3 - root_z) + 1
    along = jnp.where(below, z, 3 - z)
    if across_first:
        level = jnp.where(home, jnp.where(same, height, 1 + along), 0)
        in_line, crosses = home, y >= 0
    else:
        level = jnp.where(same, jnp.where(home, height, height - 1), along)
        in_line, crosses = y >= 0, same
    down = height + jnp.abs(z - root_z) + flag(~home)
    flags = (
        home & same,
        in_line & below,
        in_line & above,
        ~home & crosses,
        in_line & (z <= root_z) & (z > 0),
        in_line & (z >= root_z) & (z < CHIPS_Z - 1),
        home & crosses,
    )
    return level, down, [flag(f) for f in flags]


def kernel(
    a_hbm, g_hbm, out_hbm,
    roles, plan, a_t, a_in, g_in, sums, outgoing, arrived, final,
    a_sem, g_sem, outgoing_sem, arrived_sem, climb_sem, final_sem, leave_sem, other_sem,
):
    matrices, tokens, d = a_hbm.shape
    ff = g_hbm.shape[2]
    rows = d // (2 * PANELS)
    steps = ff // COLS
    panels = matrices * PANELS
    units = panels * steps
    chunks = tokens // A_STEP

    rep, me = lax.axis_index("rep"), lax.axis_index("dp")
    core = lax.rem(me, 2)
    chip = div(me, 2)
    z = lax.rem(chip, CHIPS_Z)
    y = div(chip, CHIPS_Z)
    partner = me + 1 - 2 * core
    across = me + 2 * CHIPS_Z * (1 - 2 * y)

    def device(i):
        return (rep, i)

    barrier = pltpu.get_barrier_semaphore()

    def greet(i):
        pl.semaphore_signal(barrier, inc=1, device_id=device(i), device_id_type=MESH)

    greet(partner)
    greet(across)

    @pl.when(z > 0)
    def _():
        greet(me - 2)

    @pl.when(z < CHIPS_Z - 1)
    def _():
        greet(me + 2)

    def a_copy(panel, i, slot):
        n = div(panel, PANELS)
        row = pl.multiple_of(i * A_STEP, A_STEP)
        column = pl.multiple_of((panel - n * PANELS) * (2 * rows), 2 * rows)
        return pltpu.make_async_copy(
            a_hbm.at[n, pl.ds(row, A_STEP), pl.ds(column, 2 * rows)], a_in.at[slot], a_sem.at[slot]
        )

    def g_copy(unit):
        panel = div(unit, steps)
        n = div(panel, PANELS)
        column = pl.multiple_of((unit - panel * steps) * COLS, COLS)
        slot = lax.rem(unit, 3)
        return pltpu.make_async_copy(g_hbm.at[n, :, pl.ds(column, COLS)], g_in.at[slot], g_sem.at[slot])

    def transpose(panel, i, slot):
        a_t[lax.rem(panel, 2), :, pl.ds(pl.multiple_of(i * A_STEP, A_STEP), A_STEP)] = a_in[slot].T

    def place(unit, of_core):
        panel = div(unit, steps)
        n = div(panel, PANELS)
        row = pl.multiple_of((panel - n * PANELS) * (2 * rows) + of_core * rows, rows)
        column = pl.multiple_of((unit - panel * steps) * COLS, COLS)
        return out_hbm.at[n, pl.ds(row, rows), pl.ds(column, COLS)]

    def fetch_first(i, slot):
        a_copy(jnp.int32(0), i, slot).start()

    for i in range(min(A_SLOTS, chunks)):
        fetch_first(i, i)
    g_copy(jnp.int32(0)).start()
    g_copy(jnp.int32(1)).start()

    turns = len(TREES)
    places = [role(tree, y, z) for tree in TREES]
    for turn, (_, _, flags) in enumerate(places):
        for i, value in enumerate(flags):
            roles[turn, i] = value
    for turn in range(turns):
        for k in range(STAGES + 1):
            level, down, _ = places[(turn - LAG0 - LAG * k) % turns]
            plan[turn, k] = UP * flag(level == k) + DOWN * flag(down == k)

    def role_of(unit):
        turn = lax.rem(unit, turns)
        return {name: roles[turn, i] == 1 for i, name in enumerate(FLAGS)}

    def slot_of(unit):
        return lax.rem(unit, RING)

    def pair_copy(unit):
        slot, queue = slot_of(unit), lax.rem(unit, QUEUE)
        return pltpu.make_async_remote_copy(
            src_ref=outgoing.at[queue], dst_ref=arrived.at[PAIR, slot],
            send_sem=outgoing_sem.at[queue], recv_sem=arrived_sem.at[PAIR, slot],
            device_id=device(partner), device_id_type=MESH,
        )

    def climb_copy(unit, side, to):
        slot = slot_of(unit)
        return pltpu.make_async_remote_copy(
            src_ref=arrived.at[PAIR, slot], dst_ref=arrived.at[side, slot],
            send_sem=climb_sem.at[slot], recv_sem=arrived_sem.at[side, slot],
            device_id=device(to), device_id_type=MESH,
        )

    def final_copy(unit, side, to):
        slot = slot_of(unit)
        return pltpu.make_async_remote_copy(
            src_ref=final.at[slot], dst_ref=final.at[slot],
            send_sem=leave_sem.at[side, slot], recv_sem=final_sem.at[slot],
            device_id=device(to), device_id_type=MESH,
        )

    def other_copy(unit, of_core):
        slot = slot_of(unit)
        return pltpu.make_async_remote_copy(
            src_ref=final.at[slot], dst_ref=place(unit, of_core),
            send_sem=leave_sem.at[PAIR, slot], recv_sem=other_sem.at[slot],
            device_id=device(partner), device_id_type=MESH,
        )

    def own_copy(unit):
        slot = slot_of(unit)
        return pltpu.make_async_copy(final.at[slot], place(unit, core), leave_sem.at[4, slot])

    def compute(unit):
        panel = div(unit, steps)
        step = unit - panel * steps

        @pl.when(unit + 2 < units)
        def _():
            g_copy(unit + 2).start()

        g_copy(unit).wait()
        at = lax.rem(unit, SUMS)
        sums[at] = jnp.dot(a_t[lax.rem(panel, 2)], g_in[lax.rem(unit, 3)], preferred_element_type=jnp.float32)
        outgoing[lax.rem(unit, QUEUE)] = sums[at, pl.ds(pl.multiple_of((1 - core) * rows, rows), rows), :].astype(jnp.bfloat16)
        pair_copy(unit).start()

        @pl.when(panel < panels - 1)
        def _():
            @pl.when(step < chunks)
            def _():
                a_copy(panel + 1, step, lax.rem(step, A_SLOTS)).start()

            @pl.when((step >= 1) & (step <= chunks))
            def _():
                i = step - 1
                a_copy(panel + 1, i, lax.rem(i, A_SLOTS)).wait()
                transpose(panel + 1, i, lax.rem(i, A_SLOTS))

    def climb(unit, r):
        slot = slot_of(unit)
        own = sums.at[lax.rem(unit, SUMS), pl.ds(pl.multiple_of(core * rows, rows), rows), :]
        for side, there, source in (
            (LEFT, r["from_left"], me - 2),
            (RIGHT, r["from_right"], me + 2),
            (ACROSS, r["from_across"], across),
        ):
            @pl.when(there)
            def _():
                climb_copy(unit, side, source).wait_recv()
                own[...] = own[...] + arrived[side, slot].astype(jnp.float32)

        pair_copy(unit).wait_recv()
        total = (own[...] + arrived[PAIR, slot].astype(jnp.float32)).astype(jnp.bfloat16)

        @pl.when(r["root"])
        def _():
            final[slot] = total

        @pl.when(~r["root"])
        def _():
            arrived[PAIR, slot] = total

        for side, there, to in (
            (LEFT, r["up_right"], me + 2),
            (RIGHT, r["up_left"], me - 2),
            (ACROSS, r["up_across"], across),
        ):
            @pl.when(there)
            def _():
                climb_copy(unit, side, to).start()

    def children(unit, r, act):
        for side, there, to in (
            (LEFT, r["from_left"], me - 2),
            (RIGHT, r["from_right"], me + 2),
            (ACROSS, r["from_across"], across),
        ):
            @pl.when(there)
            def _():
                act(final_copy(unit, side, to))

    def descend(unit, r):
        @pl.when(~r["root"])
        def _():
            climb_copy(unit, LEFT, partner).wait_send()
            final_copy(unit, LEFT, partner).wait_recv()

        children(unit, r, lambda copy: copy.start())
        other_copy(unit, core).start()
        own_copy(unit).start()

    def retire(unit):
        r = role_of(unit)
        children(unit, r, lambda copy: copy.wait_send())
        other_copy(unit, core).wait_send()
        own_copy(unit).wait()
        other_copy(unit, 1 - core).wait_recv()

    def first(i, carry):
        slot = lax.rem(i, A_SLOTS)
        a_copy(jnp.int32(0), i, slot).wait()
        transpose(jnp.int32(0), i, slot)

        @pl.when(i + A_SLOTS < chunks)
        def _():
            fetch_first(i + A_SLOTS, slot)

        return carry

    lax.fori_loop(0, chunks, first, 0)
    pl.semaphore_wait(barrier, 2 + flag(z > 0) + flag(z < CHIPS_Z - 1))

    def body(step, carry):
        @pl.when(step >= RING)
        def _():
            retire(step - RING)

        turn = lax.rem(step, turns)

        def stage(i, carry):
            k = STAGES - i
            unit = step - LAG0 - LAG * k
            what = plan[turn, k]

            @pl.when((what > 0) & (unit >= 0) & (unit < units))
            def _():
                r = role_of(unit)

                @pl.when(what != DOWN)
                def _():
                    climb(unit, r)

                @pl.when(what >= DOWN)
                def _():
                    descend(unit, r)

            return carry

        lax.fori_loop(0, STAGES + 1, stage, 0)

        @pl.when((step >= QUEUE) & (step < units + QUEUE))
        def _():
            pair_copy(step - QUEUE).wait_send()

        @pl.when(step < units)
        def _():
            compute(step)

        return carry

    lax.fori_loop(0, units + RING, body, 0)


HAND_SLOTS, HAND_LEAD, HAND_ROWS = 16, 8, 128


def hand_over(x_hbm, out_hbm, held, in_sem, out_sem):
    matrices, d, _ = x_hbm.shape
    pieces = [(n, pl.ds(row, HAND_ROWS)) for n in range(matrices) for row in range(0, d, HAND_ROWS)]

    def take(i):
        slot = i % HAND_SLOTS
        return pltpu.make_async_copy(x_hbm.at[pieces[i]], held.at[slot], in_sem.at[slot])

    def give(i):
        slot = i % HAND_SLOTS
        return pltpu.make_async_copy(held.at[slot], out_hbm.at[pieces[i]], out_sem.at[slot])

    for i in range(min(HAND_SLOTS, len(pieces))):
        take(i).start()
    for i in range(len(pieces) + HAND_LEAD):
        if i < len(pieces):
            take(i).wait()
            give(i).start()
        if i >= HAND_LEAD:
            give(i - HAND_LEAD).wait()
            if i - HAND_LEAD + HAND_SLOTS < len(pieces):
                take(i - HAND_LEAD + HAND_SLOTS).start()


def solution(mesh):
    def body(a, g):
        a, g = a[0], g[0]
        matrices, tokens, d = a.shape
        ff = g.shape[2]
        rows = d // (2 * PANELS)
        block = (rows, COLS)
        dma = pltpu.SemaphoreType.DMA
        flops = 2 * matrices * tokens * d * ff
        sums = pl.pallas_call(
            kernel,
            out_shape=jax.ShapeDtypeStruct((matrices, d, ff), jnp.bfloat16),
            in_specs=[pl.BlockSpec(memory_space=pl.ANY)] * 2,
            out_specs=pl.BlockSpec(memory_space=pl.ANY),
            scratch_shapes=[
                pltpu.SMEM((len(TREES), len(FLAGS)), jnp.int32),
                pltpu.SMEM((len(TREES), STAGES + 1), jnp.int32),
                pltpu.VMEM((2, 2 * rows, tokens), jnp.bfloat16),
                pltpu.VMEM((A_SLOTS, A_STEP, 2 * rows), jnp.bfloat16),
                pltpu.VMEM((3, tokens, COLS), jnp.bfloat16),
                pltpu.VMEM((SUMS, 2 * rows, COLS), jnp.float32),
                pltpu.VMEM((QUEUE, *block), jnp.bfloat16),
                pltpu.VMEM((4, RING, *block), jnp.bfloat16),
                pltpu.VMEM((RING, *block), jnp.bfloat16),
                dma((A_SLOTS,)),
                dma((3,)),
                dma((QUEUE,)),
                dma((4, RING)),
                dma((RING,)),
                dma((RING,)),
                dma((5, RING)),
                dma((RING,)),
            ],
            compiler_params=pltpu.CompilerParams(
                collective_id=0, has_side_effects=True, vmem_limit_bytes=67_043_328
            ),
            cost_estimate=pl.CostEstimate(
                flops=flops, bytes_accessed=2 * matrices * (tokens + d) * (d + ff), transcendentals=0
            ),
        )(a, g)
        return pl.pallas_call(
            hand_over,
            out_shape=jax.ShapeDtypeStruct(sums.shape, sums.dtype),
            in_specs=[pl.BlockSpec(memory_space=pl.ANY)],
            out_specs=pl.BlockSpec(memory_space=pl.ANY),
            scratch_shapes=[pltpu.VMEM((HAND_SLOTS, HAND_ROWS, ff), sums.dtype), dma((HAND_SLOTS,)), dma((HAND_SLOTS,))],
        )(sums)

    spec = P(("rep", "dp"))
    return jax.shard_map(body, mesh=mesh, in_specs=(spec, spec), out_specs=P("rep"), check_vma=False)
```

time: 616 us -> 483 us (0.78)
  Pallas kernels: 580 us -> 483 us
  local copies, waits for them, and re-layouts: 35.7 us -> 0 us
    pallas_call x1, Pallas kernels: 580 us -> 449 us  [body(): pl.pallas_call(kernel, out_shape=jax.ShapeDtypeStruct((matrices, d, ff),...]
    unnamed x1 -> x0, local copies, waits for them, and re-layouts: 35.7 us -> none
    pallas_call x0 -> x1, Pallas kernels: none -> 34.1 us  [body(): pl.pallas_call(hand_over, out_shape=jax.ShapeDtypeStruct(sums.shape, sums...]
where the time goes in v2:
time: 483 us
  Pallas kernels  483 us (100%)
    pallas_call x1, Pallas kernels, body(): pl.pallas_call(kernel, out_shape=jax.ShapeDtypeStruct((matrices, d, ff),...  449 us
    pallas_call x1, Pallas kernels, body(): pl.pallas_call(hand_over, out_shape=jax.ShapeDtypeStruct(sums.shape, sums...  34.1 us

profile of v2, /device:TPU:0, one launch (start us, length us, event | category | flops | bytes accessed | tf_op | source)
XLA Modules:
  0.0 482.9 jit_solution(5538675399127069405)
XLA Ops:
  0.0 448.8 %shard_map.28.x_hbm = bf16[4,1280,5120]{2,1,0:T(8,128)(2,1)} custom-call(bf16[4,4096,1280]{2,1,0:T(8,128)(2,1)} %bitcast.2, bf16[4,4096,5120]{2,1,0:T(8,128)(2,1)} %bitcast.1.g_hbm), custom_call_target="tpu_custom_call" | custom-call | flops 214748364800 | bytes 275251200 | tf_op jit(solution)/shard_map/pallas_call | solution.py:370
  448.8 34.1 %shard_map.29 = bf16[4,1280,5120]{2,1,0:T(8,128)(2,1)} custom-call(bf16[4,1280,5120]{2,1,0:T(8,128)(2,1)} %shard_map.28.x_hbm), custom_call_target="tpu_custom_call" | custom-call | tf_op jit(solution)/shard_map/pallas_call | solution.py:401
